TPU v7x, 32 devices: a whole 2x2x4 slice. The times are simulated.
32 devices in a mesh: dp: 8 (over z, y), tensor: 4 (over x, core).
Axes of the slice: x: 2, y: 2, z: 4, core: 2. Of those that a mesh axis runs over, the one named last changes fastest.
Arguments:
- image_rows: bfloat16 [16, 197, 768], P('dp', None, 'tensor'), may hold values from -6 to 6
- text_rows: bfloat16 [8, 512, 768], P('dp', None, 'tensor'), may hold values from -6 to 6
- pair_rows: bfloat16 [8, 711, 768], P('dp', None, 'tensor'), may hold values from -6 to 6
- text_lengths: int32 [8], P('dp'), may hold values from 128 to 512, as said below
- pair_lengths: int32 [8], P('dp'), may hold values from 128 to 512, as said below
- qkv_weight: bfloat16 [3, 768, 3, 768], P(None, None, None, 'tensor'), may hold values from -0.21875 to 0.21875
- qv_bias: bfloat16 [3, 2, 768], P(None, None, 'tensor'), may hold values from -3 to 3
- out_weight: bfloat16 [3, 768, 768], P(None, 'tensor'), may hold values from -3.5 to 3.5
- out_bias: bfloat16 [3, 768], P(None, 'tensor'), may hold values from -3 to 3
- up_weight: bfloat16 [3, 768, 3072], P(None, None, 'tensor'), may hold values from -0.21875 to 0.21875
- up_bias: bfloat16 [3, 3072], P(None, 'tensor'), may hold values from -3 to 3
- down_weight: bfloat16 [3, 3072, 768], P(None, 'tensor'), may hold values from -0.109375 to 0.109375
- down_bias: bfloat16 [3, 768], P(None, 'tensor'), may hold values from -3 to 3
- norm_gain: bfloat16 [3, 2, 768], P(None, None, 'tensor'), may hold values from 0.099609375 to 1.8984375
- norm_bias: bfloat16 [3, 2, 768], P(None, None, 'tensor'), may hold values from -3 to 3
- image_upstream: bfloat16 [16, 197, 768], P('dp', None, 'tensor'), may hold values from -6 to 6
- text_upstream: bfloat16 [8, 512, 768], P('dp', None, 'tensor'), may hold values from -6 to 6
- pair_upstream: bfloat16 [8, 711, 768], P('dp', None, 'tensor'), may hold values from -6 to 6
Outputs:
- image_out: bfloat16 [16, 197, 768], P('dp', None, 'tensor')
- text_out: bfloat16 [8, 512, 768], P('dp', None, 'tensor')
- pair_out: bfloat16 [8, 711, 768], P('dp', None, 'tensor')
- image_input_grad: bfloat16 [16, 197, 768], P('dp', None, 'tensor')
- text_input_grad: bfloat16 [8, 512, 768], P('dp', None, 'tensor')
- pair_input_grad: bfloat16 [8, 711, 768], P('dp', None, 'tensor')
- qkv_grad: float32 [3, 768, 3, 768], P(None, 'dp', None, 'tensor')
- qv_bias_grad: float32 [3, 2, 768], P(None, None, 'tensor')
- out_weight_grad: float32 [3, 768, 768], P(None, 'tensor', 'dp')
- out_bias_grad: float32 [3, 768], P(None, 'tensor')
- up_weight_grad: float32 [3, 768, 3072], P(None, 'dp', 'tensor')
- up_bias_grad: float32 [3, 3072], P(None, 'tensor')
- down_weight_grad: float32 [3, 3072, 768], P(None, 'tensor', 'dp')
- down_bias_grad: float32 [3, 768], P(None, 'tensor')
- norm_gain_grad: float32 [3, 2, 768], P(None, None, 'tensor')
- norm_bias_grad: float32 [3, 2, 768], P(None, None, 'tensor')
Inputs may be any that keep to these rules, and one draw needn't show every extreme that they name: Each text example's first text_lengths rows of 512 are valid; some example of every draw has all 512. Each pair's text rows after its 197 image rows: the first pair_lengths are valid, the rest and the two pad rows are not; some pair of every draw has all 512.
All inputs are finite; a program needn't handle non-finite values.
Results may differ from a plain program's by a relative error of at most 0.017.
Values may be sent and summed in bfloat16 or wider, within the bound.
A program may use at most 192 MiB of HBM per device.

v0:
```python
import math
import jax
import jax.numpy as jnp
from jax import lax
from jax.sharding import PartitionSpec as P

HEAD_DIM = 64
PATCHES = 196
EPSILON = 1e-06


def rounded(value):
    return lax.optimization_barrier(value.astype(jnp.bfloat16)).astype(jnp.float32)


def moments(total_count, square, feature_width):
    mean_val = total_count / feature_width
    return (mean_val, lax.rsqrt(square / feature_width - mean_val * mean_val + EPSILON))


def local_moments(value, feature_width):
    return moments(
        jnp.sum(value, axis=-1, keepdims=True),
        jnp.sum(value * value, axis=-1, keepdims=True),
        feature_width,
    )


def gather_grads(value):
    return lax.all_gather(value, "tensor", axis=2, tiled=True)


def summed_grads(value):
    return lax.psum_scatter(
        rounded(value).astype(jnp.bfloat16), "tensor", scatter_dimension=2, tiled=True
    ).astype(jnp.float32)


def norm_reverse_pass(centered_grad, standardized, inverse_deviation, feature_width):
    total_count, cross_term = lax.psum(
        (
            jnp.sum(centered_grad, axis=-1, keepdims=True),
            jnp.sum(centered_grad * standardized, axis=-1, keepdims=True),
        ),
        "tensor",
    )
    return inverse_deviation * (
        centered_grad - total_count / feature_width - standardized * cross_term / feature_width
    )


def gelu_exact(value):
    return jax.nn.gelu(value, approximate=False)


def masked_scores(queries, key_heads, key_mask, scale):
    scores = (
        jnp.einsum("elhd,emhd->ehlm", queries, key_heads, preferred_element_type=jnp.float32)
        * scale
    )
    return jnp.where(key_mask[:, None, None, :], scores, -1000000000.0)


def forward_tower(row_block, key_mask, weights, tensor_index):
    qkv_w, qv_b, out_w, out_b, up_w, up_b, down_w, down_b, gain, shift = weights
    feature_width = qkv_w.shape[0]
    share = out_w.shape[0]
    examples = row_block.shape[0]
    length = row_block.shape[1]
    head_count = share // HEAD_DIM
    scale = 1.0 / math.sqrt(HEAD_DIM)
    rows_float = row_block.astype(jnp.float32)
    whole_rows, whole_bias, whole_gain, whole_shift = (
        lax.all_gather(row_block, "tensor", axis=2, tiled=True),
        lax.all_gather(out_b, "tensor", axis=0, tiled=True),
        lax.all_gather(gain, "tensor", axis=1, tiled=True),
        lax.all_gather(shift, "tensor", axis=1, tiled=True),
    )
    whole_f = whole_rows.astype(jnp.float32)
    input_mean, input_inverse_deviation = local_moments(whole_f, feature_width)
    normed = (
        (whole_f - input_mean) * input_inverse_deviation * whole_gain[0].astype(jnp.float32)
        + whole_shift[0].astype(jnp.float32)
    ).astype(jnp.bfloat16)
    projected = jnp.einsum("eld,dcf->elcf", normed, qkv_w, preferred_element_type=jnp.float32)
    queries = (
        (projected[:, :, 0] + qv_b[0].astype(jnp.float32))
        .astype(jnp.bfloat16)
        .reshape(examples, length, head_count, HEAD_DIM)
    )
    key_heads = (
        projected[:, :, 1].astype(jnp.bfloat16).reshape(examples, length, head_count, HEAD_DIM)
    )
    value_heads = (
        (projected[:, :, 2] + qv_b[1].astype(jnp.float32))
        .astype(jnp.bfloat16)
        .reshape(examples, length, head_count, HEAD_DIM)
    )
    scores = masked_scores(queries, key_heads, key_mask, scale)
    top_score = jnp.max(scores, axis=-1, keepdims=True)
    log_total = top_score + jnp.log(jnp.sum(jnp.exp(scores - top_score), axis=-1, keepdims=True))
    probs_low = jnp.exp(scores - log_total).astype(jnp.bfloat16)
    mixed = (
        jnp.einsum("ehlm,emhd->elhd", probs_low, value_heads, preferred_element_type=jnp.float32)
        .astype(jnp.bfloat16)
        .reshape(examples, length, share)
    )
    partial_value = jnp.einsum("elf,fd->eld", mixed, out_w, preferred_element_type=jnp.float32)
    attn_full = lax.psum(rounded(partial_value).astype(jnp.bfloat16), "tensor").astype(
        jnp.float32
    ) + whole_bias.astype(jnp.float32)
    resid_full = whole_f + attn_full
    middle_mean, middle_inverse_deviation = local_moments(resid_full, feature_width)
    normed_two = (
        (resid_full - middle_mean) * middle_inverse_deviation * whole_gain[1].astype(jnp.float32)
        + whole_shift[1].astype(jnp.float32)
    ).astype(jnp.bfloat16)
    attention = lax.dynamic_slice_in_dim(attn_full, tensor_index * share, share, 2)
    residual_stream = rows_float + attention
    hidden = jnp.einsum(
        "eld,df->elf", normed_two, up_w, preferred_element_type=jnp.float32
    ) + up_b.astype(jnp.float32)
    activated = gelu_exact(hidden).astype(jnp.bfloat16)
    down_part = jnp.einsum("elf,fd->eld", activated, down_w, preferred_element_type=jnp.float32)
    feedforward = lax.psum_scatter(
        rounded(down_part).astype(jnp.bfloat16), "tensor", scatter_dimension=2, tiled=True
    ).astype(jnp.float32) + down_b.astype(jnp.float32)
    output = residual_stream + feedforward
    kept = (
        normed,
        queries,
        key_heads,
        value_heads,
        log_total,
        mixed,
        normed_two,
        hidden,
        activated,
        input_mean,
        input_inverse_deviation,
        middle_mean,
        middle_inverse_deviation,
        residual_stream,
        rows_float,
    )
    return (output, kept)


def backward_tower(upstream, weights, kept, key_mask):
    qkv_w, qv_b, out_w, out_b, up_w, up_b, down_w, down_b, gain, shift = weights
    (
        normed,
        queries,
        key_heads,
        value_heads,
        log_total,
        mixed,
        normed_two,
        hidden,
        activated,
        input_mean,
        input_inverse_deviation,
        middle_mean,
        middle_inverse_deviation,
        residual_stream,
        rows_float,
    ) = kept
    feature_width = qkv_w.shape[0]
    share = out_w.shape[0]
    examples = queries.shape[0]
    length = queries.shape[1]
    head_count = share // HEAD_DIM
    scale = 1.0 / math.sqrt(HEAD_DIM)
    gain_float = gain.astype(jnp.float32)
    output_gradient = upstream.astype(jnp.float32)
    grad_ffn = output_gradient.astype(jnp.bfloat16)
    down_bias_grad = jnp.sum(grad_ffn, axis=(0, 1), dtype=jnp.float32)
    ffn_full = gather_grads(grad_ffn)
    down_grad = jnp.einsum("elf,eld->fd", activated, ffn_full, preferred_element_type=jnp.float32)
    grad_act = jnp.einsum("eld,fd->elf", ffn_full, down_w, preferred_element_type=jnp.float32)
    grad_hidden = jax.vjp(gelu_exact, hidden)[1](grad_act)[0].astype(jnp.bfloat16)
    up_bias_grad = jnp.sum(grad_hidden, axis=(0, 1), dtype=jnp.float32)
    up_grad = jnp.einsum("eld,elf->df", normed_two, grad_hidden, preferred_element_type=jnp.float32)
    second_normed_gradient = summed_grads(
        jnp.einsum("elf,df->eld", grad_hidden, up_w, preferred_element_type=jnp.float32)
    )
    standardized_middle = (residual_stream - middle_mean) * middle_inverse_deviation
    middle_gain_grad = jnp.sum(second_normed_gradient * standardized_middle, axis=(0, 1))
    shift_mid_grad = jnp.sum(second_normed_gradient, axis=(0, 1))
    residual_gradient = output_gradient + norm_reverse_pass(
        second_normed_gradient * gain_float[1],
        standardized_middle,
        middle_inverse_deviation,
        feature_width,
    )
    grad_attn = residual_gradient.astype(jnp.bfloat16)
    out_bias_grad = jnp.sum(grad_attn, axis=(0, 1), dtype=jnp.float32)
    attn_full = gather_grads(grad_attn)
    out_grad = jnp.einsum("elf,eld->fd", mixed, attn_full, preferred_element_type=jnp.float32)
    grad_mixed = (
        jnp.einsum("eld,fd->elf", attn_full, out_w, preferred_element_type=jnp.float32)
        .astype(jnp.bfloat16)
        .reshape(examples, length, head_count, HEAD_DIM)
    )
    scores = masked_scores(queries, key_heads, key_mask, scale)
    probs_f = jnp.exp(scores - log_total)
    probs_low = probs_f.astype(jnp.bfloat16)
    grad_values = jnp.einsum(
        "ehlm,elhd->emhd", probs_low, grad_mixed, preferred_element_type=jnp.float32
    ).astype(jnp.bfloat16)
    grad_probs = jnp.einsum(
        "elhd,emhd->ehlm", grad_mixed, value_heads, preferred_element_type=jnp.float32
    )
    grad_scores = (
        probs_f * (grad_probs - jnp.sum(probs_f * grad_probs, axis=-1, keepdims=True))
    ).astype(jnp.bfloat16)
    grad_queries = (
        jnp.einsum("ehlm,emhd->elhd", grad_scores, key_heads, preferred_element_type=jnp.float32)
        * scale
    ).astype(jnp.bfloat16)
    grad_keys = (
        jnp.einsum("ehlm,elhd->emhd", grad_scores, queries, preferred_element_type=jnp.float32)
        * scale
    ).astype(jnp.bfloat16)
    grad_qkv = jnp.stack([grad_queries, grad_keys, grad_values], 2).reshape(
        examples, length, 3, share
    )
    qv_bias_grad = jnp.stack(
        [
            jnp.sum(grad_qkv[:, :, 0], axis=(0, 1), dtype=jnp.float32),
            jnp.sum(grad_qkv[:, :, 2], axis=(0, 1), dtype=jnp.float32),
        ],
        0,
    )
    qkv_grad = jnp.einsum("eld,elcf->dcf", normed, grad_qkv, preferred_element_type=jnp.float32)
    normed_gradient = summed_grads(
        jnp.einsum("elcf,dcf->eld", grad_qkv, qkv_w, preferred_element_type=jnp.float32)
    )
    standardized_input = (rows_float - input_mean) * input_inverse_deviation
    input_gain_grad = jnp.sum(normed_gradient * standardized_input, axis=(0, 1))
    shift_in_grad = jnp.sum(normed_gradient, axis=(0, 1))
    grad_input = (
        residual_gradient
        + norm_reverse_pass(
            normed_gradient * gain_float[0],
            standardized_input,
            input_inverse_deviation,
            feature_width,
        )
    ).astype(jnp.bfloat16)
    small_grads = jnp.concatenate(
        [
            qv_bias_grad,
            out_bias_grad[None],
            up_bias_grad.reshape(-1, share),
            down_bias_grad[None],
            jnp.stack([input_gain_grad, middle_gain_grad], 0),
            jnp.stack([shift_in_grad, shift_mid_grad], 0),
        ],
        0,
    )
    return (grad_input, (qkv_grad, out_grad, up_grad, down_grad, small_grads))


def per_device(
    image_rows,
    text_rows,
    pair_rows,
    text_lengths,
    pair_lengths,
    qkv_weight,
    qv_bias,
    out_weight,
    out_bias,
    up_weight,
    up_bias,
    down_weight,
    down_bias,
    norm_gain,
    norm_bias,
    image_upstream,
    text_upstream,
    pair_upstream,
):
    tensor_index = lax.axis_index("tensor")
    image_mask = jnp.ones((image_rows.shape[0], image_rows.shape[1]), dtype=bool)
    text_mask = jnp.arange(text_rows.shape[1], dtype=jnp.int32)[None, :] < text_lengths[:, None]
    pair_mask = jnp.arange(pair_rows.shape[1], dtype=jnp.int32)[None, :] < pair_lengths[:, None] + (
        PATCHES + 1
    )
    towers_in = (
        (image_rows, image_mask, image_upstream),
        (text_rows, text_mask, text_upstream),
        (pair_rows, pair_mask, pair_upstream),
    )
    params = (
        qkv_weight,
        qv_bias,
        out_weight,
        out_bias,
        up_weight,
        up_bias,
        down_weight,
        down_bias,
        norm_gain,
        norm_bias,
    )
    outputs = []
    input_grads = []
    grad_lists = ([], [], [], [], [])
    for tower_id in range(3):
        row_block, key_mask, upstream = towers_in[tower_id]
        weights = tuple((entry[tower_id] for entry in params))
        output, kept = forward_tower(row_block, key_mask, weights, tensor_index)
        outputs.append(output.astype(jnp.bfloat16))
        grad_input, grads = backward_tower(upstream, weights, kept, key_mask)
        input_grads.append(grad_input)
        for slot_id in range(5):
            grad_lists[slot_id].append(grads[slot_id])
    stacked = tuple((jnp.stack(group_list, 0) for group_list in grad_lists))
    qkv_grad, out_weight_grad, up_weight_grad, down_weight_grad = (
        lax.psum_scatter(stacked[0], "dp", scatter_dimension=1, tiled=True),
        lax.psum_scatter(stacked[1], "dp", scatter_dimension=2, tiled=True),
        lax.psum_scatter(stacked[2], "dp", scatter_dimension=1, tiled=True),
        lax.psum_scatter(stacked[3], "dp", scatter_dimension=2, tiled=True),
    )
    small_grads = lax.psum(stacked[4], "dp")
    share = out_weight.shape[1]
    hidden_share = up_weight.shape[2]
    ratio = hidden_share // share
    qv_bias_grad = small_grads[:, 0:2]
    out_bias_grad = small_grads[:, 2]
    up_bias_grad = small_grads[:, 3 : 3 + ratio].reshape(3, hidden_share)
    down_bias_grad = small_grads[:, 3 + ratio]
    norm_gain_grad = small_grads[:, 4 + ratio : 6 + ratio]
    norm_bias_grad = small_grads[:, 6 + ratio : 8 + ratio]
    return (
        outputs[0],
        outputs[1],
        outputs[2],
        input_grads[0],
        input_grads[1],
        input_grads[2],
        qkv_grad,
        qv_bias_grad,
        out_weight_grad,
        out_bias_grad,
        up_weight_grad,
        up_bias_grad,
        down_weight_grad,
        down_bias_grad,
        norm_gain_grad,
        norm_bias_grad,
    )


def solution(mesh):
    return jax.shard_map(
        per_device,
        mesh=mesh,
        in_specs=(
            P("dp", None, "tensor"),
            P("dp", None, "tensor"),
            P("dp", None, "tensor"),
            P("dp"),
            P("dp"),
            P(None, None, None, "tensor"),
            P(None, None, "tensor"),
            P(None, "tensor", None),
            P(None, "tensor"),
            P(None, None, "tensor"),
            P(None, "tensor"),
            P(None, "tensor", None),
            P(None, "tensor"),
            P(None, None, "tensor"),
            P(None, None, "tensor"),
            P("dp", None, "tensor"),
            P("dp", None, "tensor"),
            P("dp", None, "tensor"),
        ),
        out_specs=(
            P("dp", None, "tensor"),
            P("dp", None, "tensor"),
            P("dp", None, "tensor"),
            P("dp", None, "tensor"),
            P("dp", None, "tensor"),
            P("dp", None, "tensor"),
            P(None, "dp", None, "tensor"),
            P(None, None, "tensor"),
            P(None, "tensor", "dp"),
            P(None, "tensor"),
            P(None, "dp", "tensor"),
            P(None, "tensor"),
            P(None, "tensor", "dp"),
            P(None, "tensor"),
            P(None, None, "tensor"),
            P(None, None, "tensor"),
        ),
        check_vma=False,
    )
```

profile of v0, /device:TPU:0, one launch (start us, length us, event | category | flops | bytes accessed | tf_op | source)
XLA Modules:
  0.0 1013.4 jit_solution(11684703509112066378)
XLA Ops:
  8.7 7.9 all-gather.1
  16.7 5.3 fusion.178
  23.4 6.6 all-gather
  30.0 5.3 fusion.179
  35.5 8.7 all_gather.54
  56.0 12.3 %all_gather.58 = bf16[1,512,768]{1,2,0:T(8,128)(2,1)S(1)} all-gather(bf16[1,512,192]{1,2,0:T(8,128)(2,1)S(1)} %copy-done.81), channel_id=1, replica_groups=mesh['dp'=8,'tensor'=4] {'tensor'}, dimensions={2}, use_global_device_ids=true | all-gather | bytes 983040 | tf_op jit(solution)/shard_map/all_gather | solution.py:74
  68.7 6.6 all-gather.4
  75.3 5.3 fusion.174
  80.8 8.5 all-gather.3
  89.3 5.3 fusion.175
  100.1 8.3 all-reduce.8
  122.7 6.1 all-gather.7
  128.8 4.7 fusion.170
  133.7 6.6 all-gather.6
  140.3 4.7 fusion.171
  145.3 9.7 all_gather.66
  160.3 3.6 multiply_convert_fusion.5
  163.9 2.9 convert_reduce_fusion.5
  170.4 3.0 copy.174
  192.1 10.5 %all_gather.68 = bf16[1,512,768]{1,2,0:T(8,128)(2,1)} all-gather(bf16[1,512,192]{1,2,0:T(8,128)(2,1)S(1)} %copy-done.82), channel_id=1, replica_groups=mesh['dp'=8,'tensor'=4] {'tensor'}, dimensions={2}, use_global_device_ids=true | all-gather | bytes 983040 | tf_op jit(solution)/shard_map/all_gather | solution.py:30
  202.6 51.6 %all-reduce.19.cloned.1.call-done = (bf16[1,512,768]{2,1,0:T(8,128)(2,1)}, bf16[1,711,768]{2,1,0:T(8,128)(2,1)}, bf16[2,197,768]{1,0,2:T(2,128)(2,1)}) async-done(((bf16[1,512,768]{2,1,0:T(8,128)(2,1)}, bf16[1,711,768]{2,1,0:T(8,128)(2,1)}, bf16[2,197,768]{1,0,2:T(2,128)(2,1)}), (bf16[1,512,768]{2,1,0:T(8,128)(2,1)}, bf16[1,711,768]{2,1,0:T(8,128)(2,1)}, ...) | async-done | bytes 2483728 | tf_op jit(solution)/shard_map/psum | solution.py:109
  254.2 3.0 fusion.133
  257.3 6.4 multiply_convert_fusion.3
  263.7 3.1 convert_reduce_fusion.4
  267.6 3.0 fusion.34
  270.6 4.7 copy.225
  277.9 3.2 fusion.33
  281.1 4.8 copy.221
  290.5 9.1 multiply_convert_fusion.2
  299.6 5.4 convert_reduce_fusion.2
  306.0 3.3 fusion.28
  309.3 6.7 copy.229
  316.0 2.9 copy.269
  332.4 4.5 slice_reduce_fusion.4
  336.9 4.5 slice_reduce_fusion.2
  341.4 4.5 slice_reduce_fusion
  346.6 2.9 convolution_convert_fusion.7
  349.5 3.0 copy.161
  356.0 3.6 fusion.27
  359.6 6.7 copy.223
  366.3 2.9 copy.270
  389.0 11.6 %all-reduce.7 = (f32[2,197]{1,0:T(2,128)}, f32[2,197,1]{1,0,2:T(2,128)}, f32[512]{0:T(512)}, f32[1,512,1]{1,2,0:T(1,128)}, f32[711]{0:T(1024)}, /*index=5*/f32[1,711,1]{1,2,0:T(1,128)}) all-reduce(f32[2,197]{1,0:T(2,128)} %get-tuple-element.87, f32[2,197,1]{1,0,2:T(2,128)} %bitcast.503, ...), channel_id=1, replica_groups=mesh['dp'=8,'tensor'=4] {'tensor'}, use_global_device_ids=true, to_apply=%region_28.29 | all-reduce | flops 3234 | bytes 25872 | tf_op jit(solution)/shard_map/psum | solution.py:40
  401.2 3.0 convert_reduce_fusion.19
  406.0 9.1 all_gather.67
  424.3 3.0 copy.184
  427.3 3.6 convert_reduce_fusion.17
  437.5 4.1 convert_reduce_fusion.11
  443.5 9.0 all_gather.69
  464.2 2.9 copy.227
  473.2 5.3 multiply_reduce_fusion
  485.8 2.8 copy.231
  493.5 3.0 copy.235
  496.5 2.8 reshape.1243
  504.3 3.3 pad_maximum_fusion.1
  507.6 11.0 %copy.237 = f32[3,768,768]{1,0,2:T(4,128)} copy(f32[3,768,768]{2,1,0:T(8,128)} %pad_maximum_fusion.1) | data formatting | bytes 14155776
  518.5 8.2 copy.255
  535.6 9.8 copy.233
  545.4 11.3 %reshape.1241 = f32[768,1728]{1,0:T(8,128)} reshape(f32[768,3,3,192]{3,2,1,0:T(4,128)} %bitcast.422) | data formatting | bytes 10616832
  563.0 3.4 pad_maximum_fusion
  577.5 10.9 %all-reduce.6 = (f32[2,197]{1,0:T(2,128)S(1)}, f32[2,197,1]{1,0,2:T(2,128)S(1)}, f32[512]{0:T(512)S(1)}, f32[1,512,1]{1,2,0:T(1,128)S(1)}, f32[711]{0:T(1024)S(1)}, /*index=5*/f32[1,711,1]{1,2,0:T(1,128)S(1)}) all-reduce(f32[2,197]{1,0:T(2,128)S(1)} %get-tuple-element.105, ...), channel_id=1, replica_groups=mesh['dp'=8,'tensor'=4] {'tensor'}, use_global_device_ids=true, to_apply=%region_34.35 | all-reduce | flops 3234 | bytes 25872 | tf_op jit(solution)/shard_map/psum | solution.py:40
  597.3 38.3 %psum.127 = f32[3,12,192]{2,1,0:T(8,128)S(1)} all-reduce(f32[3,12,192]{2,1,0:T(8,128)S(1)} %pad_maximum_fusion.9), channel_id=1, replica_groups=mesh['dp'=8,'tensor'=4] {'dp'}, use_global_device_ids=true, to_apply=%region_85.86 | all-reduce | flops 6912 | bytes 55296 | tf_op jit(solution)/shard_map/psum | solution.py:327
  639.6 124.9 %reduce-scatter.47.cloned.1.call-done = f32[96,2304]{1,0:T(8,128)} async-done(((f32[768,2304]{1,0:T(8,128)}), f32[96,2304]{1,0:T(8,128)}) %reduce-scatter.47.cloned.1.call-update) | async-done | bytes 884752
  767.2 106.9 %reduce-scatter.43.cloned.1.call-done = f32[96,1728]{1,0:T(8,128)} async-done(((f32[768,1728]{1,0:T(8,128)}), f32[96,1728]{1,0:T(8,128)}) %reduce-scatter.43.cloned.1.call-update) | async-done | bytes 663568
  876.9 129.8 %reduce-scatter.29.cloned.1.call-done = f32[3,96,768]{2,1,0:T(8,128)} async-done(((f32[3,768,768]{2,1,0:T(8,128)}), f32[3,96,768]{2,1,0:T(8,128)}) %reduce-scatter.29.cloned.1.call-update) | async-done | bytes 884752 | tf_op jit(solution)/shard_map/reduce_scatter | solution.py:324
  (684 shorter events, 204.2 us)
Async XLA Ops:
  7.2 28.1 %copy-start.77 = (bf16[2,197,192]{1,2,0:T(8,128)(2,1)S(1)}, bf16[2,197,192]{1,2,0:T(8,128)(2,1)}, u32[]{:S(2)}) copy-start(bf16[2,197,192]{1,2,0:T(8,128)(2,1)} %param.18) | copy-start | bytes 453892
  7.2 147.8 %all-reduce.15.cloned.1.call-start = ((), (), s32[]{:S(2)}) async-start(), calls=%async_computation.10 | async-start | bytes 1228800 | tf_op jit(solution)/shard_map/psum | solution.py:109
  22.0 23.2 %copy-start.166 = (f32[768]{0:T(1024)}, f32[768]{0:T(1024)S(1)}, u32[]{:S(2)}) copy-start(f32[768]{0:T(1024)S(1)} %get-tuple-element.116) | copy-start | bytes 9220
  23.4 12.1 %copy-start.66 = (bf16[1,2,192]{1,0,2:T(2,128)(2,1)}, bf16[1,2,192]{1,0,2:T(2,128)(2,1)S(1)}, u32[]{:S(2)}) copy-start(bf16[1,2,192]{1,0,2:T(2,128)(2,1)S(1)} %copy.249) | copy-start | bytes 2308
  35.3 9.8 copy-start.168
  52.7 120.8 %all-gather.13.cloned.1.call-start = ((), (), s32[]{:S(2)}) async-start(), calls=%async_computation.11 | async-start | bytes 1474560 | tf_op jit(solution)/shard_map/all_gather | solution.py:74
  53.4 200.8 %all-reduce.19.cloned.1.call-start = ((), (), s32[]{:S(2)}) async-start(), calls=%async_computation.25 | async-start | bytes 5332992 | tf_op jit(solution)/shard_map/psum | solution.py:109
  68.6 26.4 %copy-start.11 = (bf16[1,512,768]{2,1,0:T(8,128)(2,1)}, bf16[1,512,768]{2,1,0:T(8,128)(2,1)S(1)}, u32[]{:S(2)}) copy-start(bf16[1,512,768]{2,1,0:T(8,128)(2,1)S(1)} %copy.164) | copy-start | bytes 2359300
  80.6 15.3 %copy-start.174 = (f32[768]{0:T(1024)}, f32[768]{0:T(1024)S(1)}, u32[]{:S(2)}) copy-start(f32[768]{0:T(1024)S(1)} %get-tuple-element.112) | copy-start | bytes 9220
  80.8 15.1 %copy-start.68 = (bf16[1,2,192]{1,0,2:T(2,128)(2,1)}, bf16[1,2,192]{1,0,2:T(2,128)(2,1)S(1)}, u32[]{:S(2)}) copy-start(bf16[1,2,192]{1,0,2:T(2,128)(2,1)S(1)} %copy.251) | copy-start | bytes 2308
  97.4 14.2 %copy-start.25 = (f32[1,512,1,192]{1,3,2,0:T(8,128)}, f32[1,512,1,192]{1,3,2,0:T(8,128)S(1)}, u32[]{:S(2)}) copy-start(f32[1,512,1,192]{1,3,2,0:T(8,128)S(1)} %get-tuple-element.191) | copy-start | bytes 1179652
  118.2 15.4 %copy-start.199 = (bf16[1,2,192]{2,1,0:T(2,128)(2,1)S(1)}, bf16[1,2,192]{2,1,0:T(2,128)(2,1)}, u32[]{:S(2)}) copy-start(bf16[1,2,192]{2,1,0:T(2,128)(2,1)} %get-tuple-element.209) | copy-start | bytes 2308
  121.1 24.0 %copy-start.203 = (f32[192]{0:T(256)S(1)}, f32[192]{0:T(256)}, u32[]{:S(2)}) copy-start(f32[192]{0:T(256)} %get-tuple-element.144) | copy-start | bytes 2308
  121.1 24.1 %copy-start.202 = (f32[192]{0:T(256)S(1)}, f32[192]{0:T(256)}, u32[]{:S(2)}) copy-start(f32[192]{0:T(256)} %get-tuple-element.139) | copy-start | bytes 2308
  121.1 24.1 %copy-start.83 = (bf16[2,197,192]{1,2,0:T(8,128)(2,1)S(1)}, bf16[2,197,192]{1,2,0:T(8,128)(2,1)}, u32[]{:S(2)}) copy-start(bf16[2,197,192]{1,2,0:T(8,128)(2,1)} %param.33) | copy-start | bytes 453892
  121.8 61.7 %copy-start.110 = (pred[711]{0:T(1024)(128)(4,1)}, pred[711]{0:T(1024)(128)(4,1)S(1)}, u32[]{:S(2)}) copy-start(pred[711]{0:T(1024)(128)(4,1)S(1)} %iota_compare_fusion) | copy-start | bytes 2137
  128.8 26.2 %copy-start.140 = (f32[768]{0:T(1024)S(1)}, f32[768]{0:T(1024)}, u32[]{:S(2)}) copy-start(f32[768]{0:T(1024)} %convert_element_type.887) | copy-start | bytes 9220
  133.5 44.0 %copy-start.182 = (f32[768]{0:T(1024)}, f32[768]{0:T(1024)S(1)}, u32[]{:S(2)}) copy-start(f32[768]{0:T(1024)S(1)} %get-tuple-element.108) | copy-start | bytes 9220
  133.5 156.9 %copy-start.178 = (f32[768]{0:T(1024)}, f32[768]{0:T(1024)S(1)}, u32[]{:S(2)}) copy-start(f32[768]{0:T(1024)S(1)} %get-tuple-element.109) | copy-start | bytes 9220
  133.7 24.0 %copy-start.70 = (bf16[1,2,192]{1,0,2:T(2,128)(2,1)}, bf16[1,2,192]{1,0,2:T(2,128)(2,1)S(1)}, u32[]{:S(2)}) copy-start(bf16[1,2,192]{1,0,2:T(2,128)(2,1)S(1)} %copy.253) | copy-start | bytes 2308
  145.0 32.5 %copy-start.184 = (f32[768]{0:T(1024)}, f32[768]{0:T(1024)S(1)}, u32[]{:S(2)}) copy-start(f32[768]{0:T(1024)S(1)} %get-tuple-element.106) | copy-start | bytes 9220
  145.1 145.4 %copy-start.180 = (f32[768]{0:T(1024)}, f32[768]{0:T(1024)S(1)}, u32[]{:S(2)}) copy-start(f32[768]{0:T(1024)S(1)} %get-tuple-element.107) | copy-start | bytes 9220
  145.2 35.2 %copy-start.134 = (f32[3,64]{1,0:T(4,128)}, f32[3,64]{1,0:T(4,128)S(1)}, u32[]{:S(2)}) copy-start(f32[3,64]{1,0:T(4,128)S(1)} %reshape.1120) | copy-start | bytes 2308
  145.2 41.0 %copy-start.136 = (f32[3,64]{1,0:T(4,128)}, f32[3,64]{1,0:T(4,128)S(1)}, u32[]{:S(2)}) copy-start(f32[3,64]{1,0:T(4,128)S(1)} %reshape.1119) | copy-start | bytes 2308
  145.3 12.5 %copy-start.162 = (f32[768]{0:T(1024)S(1)}, f32[768]{0:T(1024)}, u32[]{:S(2)}) copy-start(f32[768]{0:T(1024)} %get-tuple-element.117) | copy-start | bytes 9220
  145.3 12.5 %copy-start.164 = (f32[768]{0:T(1024)S(1)}, f32[768]{0:T(1024)}, u32[]{:S(2)}) copy-start(f32[768]{0:T(1024)} %get-tuple-element.115) | copy-start | bytes 9220
  145.3 12.5 %copy-start.209 = (f32[768]{0:T(1024)S(1)}, f32[768]{0:T(1024)}, u32[]{:S(2)}) copy-start(f32[768]{0:T(1024)} %get-tuple-element.137) | copy-start | bytes 9220
  191.2 108.4 %all-gather.15.cloned.1.call-start = ((), (), s32[]{:S(2)}) async-start(), calls=%async_computation.12 | async-start | bytes 1474560 | tf_op jit(solution)/shard_map/all_gather | solution.py:30
  191.8 179.9 %reduce-scatter.35.cloned.1.call-start = ((), (), s32[]{:S(2)}) async-start(), calls=%async_computation.17 | async-start | bytes 983040
  192.1 65.1 %copy-start.142 = (f32[768]{0:T(1024)}, f32[768]{0:T(1024)S(1)}, u32[]{:S(2)}) copy-start(f32[768]{0:T(1024)S(1)} %convert_element_type.888) | copy-start | bytes 9220
  277.9 97.5 %reduce-scatter.31.cloned.1.call-start = ((), (), s32[]{:S(2)}) async-start(), calls=%async_computation.15 | async-start | bytes 983040
  277.9 12.6 %copy-start.144 = (f32[768]{0:T(1024)}, f32[768]{0:T(1024)S(1)}, u32[]{:S(2)}) copy-start(f32[768]{0:T(1024)S(1)} %convert_element_type.889) | copy-start | bytes 9220
  290.4 9.2 copy-start.98
  290.4 9.2 copy-start.101
  290.4 91.2 %reduce-scatter.39.cloned.1.call-start = ((), (), s32[]{:S(2)}) async-start(), calls=%async_computation.19 | async-start | bytes 1474560
  318.9 114.5 %reduce-scatter.33.cloned.1.call-start = ((), (), s32[]{:S(2)}) async-start(), calls=%async_computation.16 | async-start | bytes 1474560
  322.7 23.3 %copy-start.161 = (bf16[3,192]{1,0:T(4,128)(2,1)S(1)}, bf16[3,192]{1,0:T(4,128)(2,1)}, u32[]{:S(2)}) copy-start(bf16[3,192]{1,0:T(4,128)(2,1)} %param.30) | copy-start | bytes 3460
  324.6 112.9 %copy-start.9 = (bf16[1,711,192]{2,1,0:T(8,128)(2,1)}, bf16[1,711,192]{2,1,0:T(8,128)(2,1)S(1)}, u32[]{:S(2)}) copy-start(bf16[1,711,192]{2,1,0:T(8,128)(2,1)S(1)} %copy.168) | copy-start | bytes 819076
  336.9 32.3 %copy-start.138 = (f32[192]{0:T(256)}, f32[192]{0:T(256)S(1)}, u32[]{:S(2)}) copy-start(f32[192]{0:T(256)S(1)} %get-tuple-element.135) | copy-start | bytes 2308
  369.2 100.9 %all-gather.17.cloned.1.call-start = ((), (), s32[]{:S(2)}) async-start(), calls=%async_computation.13 | async-start | bytes 1474560 | tf_op jit(solution)/shard_map/all_gather | solution.py:30
  369.3 9.8 copy-start.128
  369.3 9.8 copy-start.131
  371.7 7.5 copy-start.153
  401.2 15.3 %copy-start.121 = (f32[2,197]{1,0:T(2,128)}, f32[2,197]{1,0:T(2,128)S(1)}, u32[]{:S(2)}) copy-start(f32[2,197]{1,0:T(2,128)S(1)} %multiply_bitcast_fusion.1) | copy-start | bytes 4732
  406.0 10.6 %copy-start.2 = (f32[2,3,197,197]{2,3,1,0:T(8,128)S(1)}, f32[2,3,197,197]{2,3,1,0:T(8,128)}, u32[]{:S(2)}) copy-start(f32[2,3,197,197]{2,3,1,0:T(8,128)} %copy-done.1) | copy-start | bytes 2794252
  406.0 10.6 %copy-start.32 = (f32[2,197,1,192]{1,3,2,0:T(8,128)S(1)}, f32[2,197,1,192]{1,3,2,0:T(8,128)}, u32[]{:S(2)}) copy-start(f32[2,197,1,192]{1,3,2,0:T(8,128)} %copy-done.31) | copy-start | bytes 907780
  430.9 6.6 copy-start.186
  430.9 6.6 copy-start.200
  443.5 125.9 %all-reduce.17.cloned.1.call-start = ((), (), s32[]{:S(2)}) async-start(), calls=%async_computation.24 | async-start | bytes 3145728
  443.5 11.4 %copy-start.5 = (bf16[3,512,512]{1,2,0:T(8,128)(2,1)S(1)}, bf16[3,512,512]{1,2,0:T(8,128)(2,1)}, u32[]{:S(2)}) copy-start(bf16[3,512,512]{1,2,0:T(8,128)(2,1)} %fusion.14) | copy-start | bytes 4718596
  459.6 112.8 %reduce-scatter.37.cloned.1.call-start = ((), (), s32[]{:S(2)}) async-start(), calls=%async_computation.18 | async-start | bytes 983040
  469.9 104.9 %reduce-scatter.41.cloned.1.call-start = ((), (), s32[]{:S(2)}) async-start(), calls=%async_computation.20 | async-start | bytes 1474560
  473.2 9.7 copy-start.58
  489.9 147.6 %reduce-scatter.45.cloned.1.call-start = ((), (), s32[]{:S(2)}) async-start(), calls=%async_computation.22 | async-start | bytes 2211840
  499.4 265.1 %reduce-scatter.47.cloned.1.call-start = ((), (), s32[]{:S(2)}) async-start(), calls=%async_computation.23 | async-start | bytes 7962624
  526.8 347.3 %reduce-scatter.43.cloned.1.call-start = ((), (), s32[]{:S(2)}) async-start(), calls=%async_computation.21 | async-start | bytes 6193152
  556.8 449.9 %reduce-scatter.29.cloned.1.call-start = ((), (), s32[]{:S(2)}) async-start(), calls=%async_computation.14 | async-start | bytes 7962624 | tf_op jit(solution)/shard_map/reduce_scatter | solution.py:324
  574.0 14.4 %copy-start.35 = (bf16[2,197,192]{2,1,0:T(8,128)(2,1)S(1)}, bf16[2,197,192]{2,1,0:T(8,128)(2,1)}, u32[]{:S(2)}) copy-start(bf16[2,197,192]{2,1,0:T(8,128)(2,1)} %copy.175) | copy-start | bytes 453892
  574.0 14.4 %copy-start.47 = (bf16[2,197,192]{2,1,0:T(8,128)(2,1)S(1)}, bf16[2,197,192]{2,1,0:T(8,128)(2,1)}, u32[]{:S(2)}) copy-start(bf16[2,197,192]{2,1,0:T(8,128)(2,1)} %copy.173) | copy-start | bytes 453892
  574.0 14.4 %copy-start.122 = (f32[2,197]{1,0:T(2,128)S(1)}, f32[2,197]{1,0:T(2,128)}, u32[]{:S(2)}) copy-start(f32[2,197]{1,0:T(2,128)} %copy-done.121) | copy-start | bytes 4732
  574.0 14.4 %copy-start.139 = (f32[192]{0:T(256)S(1)}, f32[192]{0:T(256)}, u32[]{:S(2)}) copy-start(f32[192]{0:T(256)} %copy-done.138) | copy-start | bytes 2308
  574.1 14.4 %copy-start.159 = (f32[2,197]{1,0:T(2,128)S(1)}, f32[2,197]{1,0:T(2,128)}, u32[]{:S(2)}) copy-start(f32[2,197]{1,0:T(2,128)} %get-tuple-element.154) | copy-start | bytes 4732
  574.1 14.4 %copy-start.198 = (f32[1,192]{1,0:T(1,128)S(1)}, f32[1,192]{1,0:T(1,128)}, u32[]{:S(2)}) copy-start(f32[1,192]{1,0:T(1,128)} %get-tuple-element.216) | copy-start | bytes 2308
  576.9 17.7 %copy-start.46 = (f32[1,512,192]{2,1,0:T(8,128)S(1)}, f32[1,512,192]{2,1,0:T(8,128)}, u32[]{:S(2)}) copy-start(f32[1,512,192]{2,1,0:T(8,128)} %get-tuple-element.172) | copy-start | bytes 1179652
  (176 other events, 409.9 us)
Sparse Core Ops, SparseCore 0:
  52.8 36.7 all-reduce.14
  91.1 18.1 all-gather.12
  191.3 62.8 all-reduce.18
  255.6 17.4 all-gather.14
  278.0 23.3 reduce-scatter.34
  303.8 23.2 reduce-scatter.30
  329.6 25.6 reduce-scatter.38
  369.3 25.7 reduce-scatter.32
  443.6 17.4 all-gather.16
  464.5 42.8 all-reduce.16
  509.9 23.2 reduce-scatter.36
  535.6 25.6 reduce-scatter.40
  564.8 67.8 reduce-scatter.44
  636.2 128.2 reduce-scatter.46
  768.0 106.0 reduce-scatter.42
  878.2 128.5 reduce-scatter.28
where the time goes:
time: 1030 us; the launch traced here: 1010 us
  waiting for transfers between devices  415 us (40%)
  local copies, waits for them, and re-layouts  204 us (20%)
  blocking collectives  171 us (17%)
  matrix products  106 us (10%)
  other arithmetic  96.2 us (9%)
  between operations  19.5 us (2%)
    unnamed x26, waiting for transfers between devices  233 us
    unnamed x514, local copies, waits for them, and re-layouts  160 us
    reduce_scatter x1, waiting for transfers between devices, per_device(): lax.psum_scatter(stacked[2], 'dp', scatter_dimension=1, tiled=True)  130 us
    psum x2, waiting for transfers between devices, forward_tower(): lax.psum(rounded(partial_value).astype(jnp.bfloat16), 'tensor')  51.6 us
    all_gather x4, blocking collectives, gather_grads(): return lax.all_gather(value, 'tensor', axis=2, tiled=True)  38.4 us
    psum x1, blocking collectives, per_device(): small_grads = lax.psum(stacked[4], 'dp')  38.3 us
    psum x2, blocking collectives, norm_reverse_pass(): lax.psum((jnp.sum(centered_grad, axis=-1, keepdims=True), jnp.sum(centere...  22.5 us
    all_gather x3, blocking collectives, forward_tower(): lax.all_gather(gain, 'tensor', axis=1, tiled=True)  21.7 us
  transfers between devices with their start and end apart: 16, of which 4 were waited for; matrix products, arithmetic and copies ran while one was open for 34% of the time, Pallas kernels for 0%

commit v1 on v0

--- a/solution.py
+++ b/solution.py
@@ -9,6 +9,22 @@
 EPSILON = 1e-06
 
 
+def collect(x, axis, dim):
+    ways, here, step = (lax.axis_size(axis), lax.axis_index(axis), x.shape[dim])
+    shape = [n * ways if d == dim else n for d, n in enumerate(x.shape)]
+    full = lax.dynamic_update_slice_in_dim(jnp.zeros(shape, x.dtype), x, here * step, axis=dim)
+    going_up = going_down = x
+    for far in range(1, ways // 2 + 1):
+        going_up = lax.ppermute(going_up, axis, [(d, (d + 1) % ways) for d in range(ways)])
+        full = lax.dynamic_update_slice_in_dim(full, going_up, (here - far) % ways * step, axis=dim)
+        if 2 * far < ways:
+            going_down = lax.ppermute(going_down, axis, [(d, (d - 1) % ways) for d in range(ways)])
+            full = lax.dynamic_update_slice_in_dim(
+                full, going_down, (here + far) % ways * step, axis=dim
+            )
+    return full
+
+
 def rounded(value):
     return lax.optimization_barrier(value.astype(jnp.bfloat16)).astype(jnp.float32)
 
@@ -27,7 +43,7 @@
 
 
 def gather_grads(value):
-    return lax.all_gather(value, "tensor", axis=2, tiled=True)
+    return collect(value, "tensor", 2)
 
 
 def summed_grads(value):

time: 1030 us -> 1090 us (1.058)
  local copies, waits for them, and re-layouts: 204 us -> 295 us
  waiting for transfers between devices: 415 us -> 386 us
  blocking collectives: 171 us -> 145 us
  starting transfers between devices: 1.85 us -> 14.1 us
    dynamic_update_slice x0 -> x24, local copies, waits for them, and re-layouts: none -> 82.6 us  [the longest x12 39.2 us: collect(): lax.dynamic_update_slice_in_dim(full, going_up, (here - far) % ways * ste...]
    all_gather x4 -> x0, blocking collectives: 38.4 us -> none  [gather_grads(): return lax.all_gather(value, 'tensor', axis=2, tiled=True)]
    unnamed x26 -> x24, waiting for transfers between devices: 233 us -> 206 us
    another operation x0 -> x14, local copies, waits for them, and re-layouts: none -> 16.1 us
    psum x2, waiting for transfers between devices: 51.6 us -> 37.9 us  [forward_tower(): lax.psum(rounded(partial_value).astype(jnp.bfloat16), 'tensor')]
    ppermute x0 -> x18, starting transfers between devices: none -> 12.7 us  [the longest x6 9.61 us: collect(): lax.ppermute(going_down, axis, [(d, (d - 1) % ways) for d in range(ways)])]
    ppermute x0 -> x18, waiting for transfers between devices: none -> 12.2 us  [the longest x12 12.2 us: collect(): lax.ppermute(going_up, axis, [(d, (d + 1) % ways) for d in range(ways)])]
    unnamed x514 -> x510, local copies, waits for them, and re-layouts: 160 us -> 155 us
  transfers between devices with their start and end apart: 16 -> 32, of which waited for: 4 -> 6; matrix products, arithmetic and copies ran while one was open for 34% -> 40% of each run, Pallas kernels for 0% -> 0%
where the time goes in v1:
time: 1090 us; the launch traced here: 1070 us
  waiting for transfers between devices  386 us (35%)
  local copies, waits for them, and re-layouts  295 us (27%)
  blocking collectives  145 us (13%)
  matrix products  114 us (10%)
  other arithmetic  97.3 us (9%)
  between operations  19.8 us (2%)
  starting transfers between devices  14.1 us (1%)
    unnamed x24, waiting for transfers between devices  206 us
    unnamed x510, local copies, waits for them, and re-layouts  155 us
    reduce_scatter x1, waiting for transfers between devices, per_device(): lax.psum_scatter(stacked[2], 'dp', scatter_dimension=1, tiled=True)  130 us
    dynamic_update_slice x12, local copies, waits for them, and re-layouts, collect(): lax.dynamic_update_slice_in_dim(full, going_up, (here - far) % ways * ste...  39.2 us
    psum x1, blocking collectives, per_device(): small_grads = lax.psum(stacked[4], 'dp')  38.6 us
    psum x2, waiting for transfers between devices, forward_tower(): lax.psum(rounded(partial_value).astype(jnp.bfloat16), 'tensor')  37.9 us
    all_gather x3, blocking collectives, forward_tower(): lax.all_gather(shift, 'tensor', axis=1, tiled=True)  30.6 us
    psum x2, blocking collectives, norm_reverse_pass(): lax.psum((jnp.sum(centered_grad, axis=-1, keepdims=True), jnp.sum(centere...  26.5 us
  transfers between devices with their start and end apart: 32, of which 6 were waited for; matrix products, arithmetic and copies ran while one was open for 40% of the time, Pallas kernels for 0%

profile of v1, /device:TPU:0, one launch (start us, length us, event | category | flops | bytes accessed | tf_op | source)
XLA Modules:
  0.0 1071.7 jit_solution(18132837572147600012)
XLA Ops:
  8.2 7.9 all-gather.1
  16.1 5.3 fusion.168
  22.3 6.6 all-gather
  28.9 5.3 fusion.169
  34.4 8.7 all_gather.36
  55.5 12.6 %all_gather.40 = bf16[1,512,768]{1,2,0:T(8,128)(2,1)S(1)} all-gather(bf16[1,512,192]{1,2,0:T(8,128)(2,1)S(1)} %copy-done.79), channel_id=1, replica_groups=mesh['dp'=8,'tensor'=4] {'tensor'}, dimensions={2}, use_global_device_ids=true | all-gather | bytes 983040 | tf_op jit(solution)/shard_map/all_gather | solution.py:90
  68.6 6.6 all-gather.4
  75.2 5.3 fusion.164
  80.6 7.9 all-gather.3
  88.5 5.3 fusion.165
  108.9 16.0 %all-gather.7 = bf16[1,2,768]{1,0,2:T(2,128)(2,1)S(1)} all-gather(bf16[1,2,192]{1,0,2:T(2,128)(2,1)S(1)} %copy.288), channel_id=9, replica_groups=mesh['dp'=8,'tensor'=4] {'tensor'}, dimensions={2}, use_global_device_ids=true | all-gather | bytes 3840 | tf_op jit(solution)/shard_map/all_gather | solution.py:93
  124.9 5.4 fusion.160
  130.5 6.6 all-gather.6
  137.0 5.3 fusion.161
  146.1 7.4 all-reduce.8
  168.4 4.3 fusion.171
  174.9 4.8 multiply_convert_fusion.5
  209.9 4.9 collective-permute-done.6
  216.9 3.8 dynamic_update_slice.96
  226.6 3.8 dynamic_update_slice.98
  231.5 3.3 dynamic_update_slice.99
  234.8 37.9 %all-reduce.19.cloned.1.call-done = (bf16[1,512,768]{2,1,0:T(8,128)(2,1)}, bf16[1,711,768]{2,1,0:T(8,128)(2,1)}, bf16[2,197,768]{1,0,2:T(2,128)(2,1)}) async-done(((bf16[1,512,768]{2,1,0:T(8,128)(2,1)}, bf16[1,711,768]{2,1,0:T(8,128)(2,1)}, bf16[2,197,768]{1,0,2:T(2,128)(2,1)}), (bf16[1,512,768]{2,1,0:T(8,128)(2,1)}, bf16[1,711,768]{2,1,0:T(8,128)(2,1)}, ...) | async-done | bytes 2483728 | tf_op jit(solution)/shard_map/psum | solution.py:125
  275.7 6.4 multiply_convert_fusion.3
  289.1 4.8 copy.259
  298.2 7.3 collective-permute-done.12
  307.7 4.6 dynamic_update_slice.104
  315.3 4.3 dynamic_update_slice.105
  319.7 5.1 dynamic_update_slice.106
  325.9 4.4 dynamic_update_slice.107
  333.5 4.8 copy.255
  342.8 8.4 multiply_convert_fusion.2
  351.2 3.5 convert_reduce_fusion.2
  355.8 3.4 fusion.28
  359.2 6.7 copy.263
  380.3 4.5 slice_reduce_fusion.4
  384.8 4.5 slice_reduce_fusion.2
  389.9 3.6 fusion.27
  393.6 6.7 copy.257
  403.2 4.5 slice_reduce_fusion
  431.0 12.7 %all-reduce.7 = (f32[2,197]{1,0:T(2,128)}, f32[2,197,1]{1,0,2:T(2,128)}, f32[512]{0:T(512)}, f32[1,512,1]{1,2,0:T(1,128)}, f32[711]{0:T(1024)}, /*index=5*/f32[1,711,1]{1,2,0:T(1,128)}) all-reduce(f32[2,197]{1,0:T(2,128)} %get-tuple-element.87, f32[2,197,1]{1,0,2:T(2,128)} %bitcast.505, ...), channel_id=1, replica_groups=mesh['dp'=8,'tensor'=4] {'tensor'}, use_global_device_ids=true, to_apply=%region_28.29 | all-reduce | flops 3234 | bytes 25872 | tf_op jit(solution)/shard_map/psum | solution.py:56
  449.7 3.6 convert_reduce_fusion.17
  459.6 4.1 convert_reduce_fusion.11
  475.1 3.5 dynamic_update_slice.100
  479.7 4.6 dynamic_update_slice.108
  492.3 3.9 dynamic_update_slice.102
  497.1 4.5 dynamic_update_slice.109
  501.7 5.1 dynamic_update_slice.110
  520.8 3.4 dynamic_update_slice.103
  537.8 4.7 dynamic_update_slice.111
  544.3 3.8 convert_reduce_fusion.15
  548.2 5.3 multiply_reduce_fusion
  558.9 3.3 fusion.29
  562.2 5.7 copy.265
  588.4 9.8 copy.267
  598.2 11.4 %reshape.1309 = f32[768,1728]{1,0:T(8,128)} reshape(f32[768,3,3,192]{3,2,1,0:T(4,128)} %bitcast.424) | data formatting | bytes 10616832
  615.5 3.3 pad_maximum_fusion.1
  618.8 11.0 %copy.271 = f32[3,768,768]{1,0,2:T(4,128)} copy(f32[3,768,768]{2,1,0:T(8,128)} %pad_maximum_fusion.1) | data formatting | bytes 14155776
  629.9 8.2 copy.289
  644.6 3.3 pad_maximum_fusion
  659.1 13.8 %all-reduce.6 = (f32[2,197]{1,0:T(2,128)S(1)}, f32[2,197,1]{1,0,2:T(2,128)S(1)}, f32[512]{0:T(512)S(1)}, f32[1,512,1]{1,2,0:T(1,128)S(1)}, f32[711]{0:T(1024)S(1)}, /*index=5*/f32[1,711,1]{1,2,0:T(1,128)S(1)}) all-reduce(f32[2,197]{1,0:T(2,128)S(1)} %get-tuple-element.105, ...), channel_id=1, replica_groups=mesh['dp'=8,'tensor'=4] {'tensor'}, use_global_device_ids=true, to_apply=%region_34.35 | all-reduce | flops 3234 | bytes 25872 | tf_op jit(solution)/shard_map/psum | solution.py:56
  680.9 38.6 %psum.127 = f32[3,12,192]{2,1,0:T(8,128)S(1)} all-reduce(f32[3,12,192]{2,1,0:T(8,128)S(1)} %pad_maximum_fusion.9), channel_id=1, replica_groups=mesh['dp'=8,'tensor'=4] {'dp'}, use_global_device_ids=true, to_apply=%region_85.86 | all-reduce | flops 6912 | bytes 55296 | tf_op jit(solution)/shard_map/psum | solution.py:343
  723.4 76.6 %reduce-scatter.43.cloned.1.call-done = f32[96,1728]{1,0:T(8,128)} async-done(((f32[768,1728]{1,0:T(8,128)}), f32[96,1728]{1,0:T(8,128)}) %reduce-scatter.43.cloned.1.call-update) | async-done | bytes 663568
  802.9 129.4 %reduce-scatter.47.cloned.1.call-done = f32[96,2304]{1,0:T(8,128)} async-done(((f32[768,2304]{1,0:T(8,128)}), f32[96,2304]{1,0:T(8,128)}) %reduce-scatter.47.cloned.1.call-update) | async-done | bytes 884752
  935.0 129.8 %reduce-scatter.29.cloned.1.call-done = f32[3,96,768]{2,1,0:T(8,128)} async-done(((f32[3,768,768]{2,1,0:T(8,128)}), f32[3,96,768]{2,1,0:T(8,128)}) %reduce-scatter.29.cloned.1.call-update) | async-done | bytes 884752 | tf_op jit(solution)/shard_map/reduce_scatter | solution.py:340
  (744 shorter events, 285.8 us)
Async XLA Ops:
  7.2 27.0 %copy-start.73 = (bf16[2,197,192]{1,2,0:T(8,128)(2,1)S(1)}, bf16[2,197,192]{1,2,0:T(8,128)(2,1)}, u32[]{:S(2)}) copy-start(bf16[2,197,192]{1,2,0:T(8,128)(2,1)} %param.18) | copy-start | bytes 453892
  7.2 158.3 %all-reduce.15.cloned.1.call-start = ((), (), s32[]{:S(2)}) async-start(), calls=%async_computation.10 | async-start | bytes 1228800 | tf_op jit(solution)/shard_map/psum | solution.py:125
  21.4 22.6 %copy-start.164 = (f32[768]{0:T(1024)}, f32[768]{0:T(1024)S(1)}, u32[]{:S(2)}) copy-start(f32[768]{0:T(1024)S(1)} %get-tuple-element.116) | copy-start | bytes 9220
  22.3 12.1 %copy-start.62 = (bf16[1,2,192]{1,0,2:T(2,128)(2,1)}, bf16[1,2,192]{1,0,2:T(2,128)(2,1)S(1)}, u32[]{:S(2)}) copy-start(bf16[1,2,192]{1,0,2:T(2,128)(2,1)S(1)} %copy.283) | copy-start | bytes 2308
  34.2 9.8 copy-start.166
  51.1 138.1 %all-gather.11.cloned.1.call-start = ((), (), s32[]{:S(2)}) async-start(), calls=%async_computation.11 | async-start | bytes 1474560 | tf_op jit(solution)/shard_map/all_gather | solution.py:90
  51.1 107.7 %collective-permute-start = (bf16[2,197,192]{1,2,0:T(8,128)(2,1)}, bf16[2,197,192]{1,2,0:T(8,128)(2,1)}, u32[]{:S(2)}, u32[]{:S(2)}) collective-permute-start(bf16[2,197,192]{1,2,0:T(8,128)(2,1)} %param.33), channel_id=1, source_target_pairs={{0,1},{1,2},{2,3},{3,0},{4,5},{5,6},{6,7},{7,4},{8,9},{9,10},{10,1... | collective-permute-start | bytes 453896 | tf_op jit(solution)/shard_map/ppermute | solution.py:18
  51.5 110.4 %collective-permute-start.1 = (bf16[2,197,192]{1,2,0:T(8,128)(2,1)}, bf16[2,197,192]{1,2,0:T(8,128)(2,1)}, u32[]{:S(2)}, u32[]{:S(2)}) collective-permute-start(bf16[2,197,192]{1,2,0:T(8,128)(2,1)} %param.33), channel_id=1, source_target_pairs={{0,3},{1,0},{2,1},{3,2},{4,7},{5,4},{6,5},{7,6},{8,11},{9,8},{10,9... | collective-permute-start | bytes 453896 | tf_op jit(solution)/shard_map/ppermute | solution.py:21
  53.0 219.8 %all-reduce.19.cloned.1.call-start = ((), (), s32[]{:S(2)}) async-start(), calls=%async_computation.23 | async-start | bytes 5332992 | tf_op jit(solution)/shard_map/psum | solution.py:125
  68.4 25.8 %copy-start.7 = (bf16[1,512,768]{2,1,0:T(8,128)(2,1)}, bf16[1,512,768]{2,1,0:T(8,128)(2,1)S(1)}, u32[]{:S(2)}) copy-start(bf16[1,512,768]{2,1,0:T(8,128)(2,1)S(1)} %copy.191) | copy-start | bytes 2359300
  80.4 14.6 %copy-start.176 = (f32[768]{0:T(1024)}, f32[768]{0:T(1024)S(1)}, u32[]{:S(2)}) copy-start(f32[768]{0:T(1024)S(1)} %get-tuple-element.112) | copy-start | bytes 9220
  80.6 14.5 %copy-start.64 = (bf16[1,2,192]{1,0,2:T(2,128)(2,1)}, bf16[1,2,192]{1,0,2:T(2,128)(2,1)S(1)}, u32[]{:S(2)}) copy-start(bf16[1,2,192]{1,0,2:T(2,128)(2,1)S(1)} %copy.285) | copy-start | bytes 2308
  108.8 35.3 %copy-start.209 = (u32[32]{0:T(128)S(1)}, u32[32]{0:T(128)}, u32[]{:S(2)}) copy-start(u32[32]{0:T(128)} %constant.272) | copy-start | bytes 388
  108.8 36.6 %copy-start.212 = (bf16[192]{0:T(256)(128)(2,1)S(1)}, bf16[192]{0:T(256)(128)(2,1)}, u32[]{:S(2)}) copy-start(bf16[192]{0:T(256)(128)(2,1)} %get-tuple-element.146) | copy-start | bytes 1156
  108.8 36.8 %copy-start.211 = (bf16[192]{0:T(256)(128)(2,1)S(1)}, bf16[192]{0:T(256)(128)(2,1)}, u32[]{:S(2)}) copy-start(bf16[192]{0:T(256)(128)(2,1)} %get-tuple-element.147) | copy-start | bytes 1156
  108.8 37.0 %copy-start.210 = (bf16[192]{0:T(256)(128)(2,1)S(1)}, bf16[192]{0:T(256)(128)(2,1)}, u32[]{:S(2)}) copy-start(bf16[192]{0:T(256)(128)(2,1)} %get-tuple-element.145) | copy-start | bytes 1156
  108.8 45.2 %copy-start.199 = (f32[192]{0:T(256)S(1)}, f32[192]{0:T(256)}, u32[]{:S(2)}) copy-start(f32[192]{0:T(256)} %get-tuple-element.144) | copy-start | bytes 2308
  108.9 45.9 %copy-start.198 = (f32[192]{0:T(256)S(1)}, f32[192]{0:T(256)}, u32[]{:S(2)}) copy-start(f32[192]{0:T(256)} %get-tuple-element.139) | copy-start | bytes 2308
  130.3 27.9 %copy-start.142 = (bf16[3,768]{1,0:T(4,128)(2,1)S(1)}, bf16[3,768]{1,0:T(4,128)(2,1)}, u32[]{:S(2)}) copy-start(bf16[3,768]{1,0:T(4,128)(2,1)} %param.28) | copy-start | bytes 13828
  130.4 12.5 %copy-start.66 = (bf16[1,2,192]{1,0,2:T(2,128)(2,1)}, bf16[1,2,192]{1,0,2:T(2,128)(2,1)S(1)}, u32[]{:S(2)}) copy-start(bf16[1,2,192]{1,0,2:T(2,128)(2,1)S(1)} %copy.287) | copy-start | bytes 2308
  144.0 24.3 %copy-start.32 = (bf16[2,197,192]{2,1,0:T(8,128)(2,1)}, bf16[2,197,192]{2,1,0:T(8,128)(2,1)S(1)}, u32[]{:S(2)}) copy-start(bf16[2,197,192]{2,1,0:T(8,128)(2,1)S(1)} %copy.200) | copy-start | bytes 453892
  165.5 7.2 collective-permute-start.2
  207.4 206.3 %reduce-scatter.35.cloned.1.call-start = ((), (), s32[]{:S(2)}) async-start(), calls=%async_computation.15 | async-start | bytes 983040
  207.4 7.4 collective-permute-start.6
  208.6 13.1 %collective-permute-start.7 = (bf16[1,512,192]{1,2,0:T(8,128)(2,1)}, bf16[1,512,192]{1,2,0:T(8,128)(2,1)}, u32[]{:S(2)}, u32[]{:S(2)}) collective-permute-start(bf16[1,512,192]{1,2,0:T(8,128)(2,1)} %param.34), channel_id=1, source_target_pairs={{0,3},{1,0},{2,1},{3,2},{4,7},{5,4},{6,5},{7,6},{8,11},{9,8},{10,9... | collective-permute-start | bytes 589832 | tf_op jit(solution)/shard_map/ppermute | solution.py:21
  214.8 15.7 %collective-permute-start.8 = (bf16[1,512,192]{1,2,0:T(8,128)(2,1)}, bf16[1,512,192]{1,2,0:T(8,128)(2,1)}, u32[]{:S(2)}, u32[]{:S(2)}) collective-permute-start(bf16[1,512,192]{1,2,0:T(8,128)(2,1)} %collective-permute-done.6), channel_id=1, source_target_pairs={{0,1},{1,2},{2,3},{3,0},{4,5},{5,6},{6,7},{7,4},{8,9},{9,10},{10,1... | collective-permute-start | bytes 589832 | tf_op jit(solution)/shard_map/ppermute | solution.py:18
  214.8 60.9 %copy-start.138 = (f32[768]{0:T(1024)}, f32[768]{0:T(1024)S(1)}, u32[]{:S(2)}) copy-start(f32[768]{0:T(1024)S(1)} %convert_element_type.888) | copy-start | bytes 9220
  293.9 11.6 %copy-start.207 = (bf16[768]{0:T(1024)(128)(2,1)S(1)}, bf16[768]{0:T(1024)(128)(2,1)}, u32[]{:S(2)}) copy-start(bf16[768]{0:T(1024)(128)(2,1)} %get-tuple-element.162) | copy-start | bytes 4612
  296.4 121.0 %reduce-scatter.31.cloned.1.call-start = ((), (), s32[]{:S(2)}) async-start(), calls=%async_computation.13 | async-start | bytes 983040
  296.4 9.1 collective-permute-start.12
  296.5 17.0 %collective-permute-start.13 = (bf16[1,711,192]{1,2,0:T(8,128)(2,1)}, bf16[1,711,192]{1,2,0:T(8,128)(2,1)}, u32[]{:S(2)}, u32[]{:S(2)}) collective-permute-start(bf16[1,711,192]{1,2,0:T(8,128)(2,1)} %param.35), channel_id=1, source_target_pairs={{0,3},{1,0},{2,1},{3,2},{4,7},{5,4},{6,5},{7,6},{8,11},{9,8},{10,9... | collective-permute-start | bytes 819080 | tf_op jit(solution)/shard_map/ppermute | solution.py:21
  305.5 19.3 %collective-permute-start.14 = (bf16[1,711,192]{1,2,0:T(8,128)(2,1)}, bf16[1,711,192]{1,2,0:T(8,128)(2,1)}, u32[]{:S(2)}, u32[]{:S(2)}) collective-permute-start(bf16[1,711,192]{1,2,0:T(8,128)(2,1)} %collective-permute-done.12), channel_id=1, source_target_pairs={{0,1},{1,2},{2,3},{3,0},{4,5},{5,6},{6,7},{7,4},{8,9},{9,10},{10,1... | collective-permute-start | bytes 819080 | tf_op jit(solution)/shard_map/ppermute | solution.py:18
  305.5 37.3 %copy-start.140 = (f32[768]{0:T(1024)}, f32[768]{0:T(1024)S(1)}, u32[]{:S(2)}) copy-start(f32[768]{0:T(1024)S(1)} %convert_element_type.889) | copy-start | bytes 9220
  342.7 80.9 %reduce-scatter.39.cloned.1.call-start = ((), (), s32[]{:S(2)}) async-start(), calls=%async_computation.17 | async-start | bytes 1474560
  368.9 86.7 %reduce-scatter.33.cloned.1.call-start = ((), (), s32[]{:S(2)}) async-start(), calls=%async_computation.14 | async-start | bytes 1474560
  369.9 19.4 %copy-start.159 = (bf16[3,192]{1,0:T(4,128)(2,1)S(1)}, bf16[3,192]{1,0:T(4,128)(2,1)}, u32[]{:S(2)}) copy-start(bf16[3,192]{1,0:T(4,128)(2,1)} %param.30) | copy-start | bytes 3460
  384.8 26.4 %copy-start.134 = (f32[192]{0:T(256)}, f32[192]{0:T(256)S(1)}, u32[]{:S(2)}) copy-start(f32[192]{0:T(256)S(1)} %get-tuple-element.135) | copy-start | bytes 2308
  403.1 248.0 %all-reduce.17.cloned.1.call-start = ((), (), s32[]{:S(2)}) async-start(), calls=%async_computation.22 | async-start | bytes 3145728
  411.2 9.9 copy-start.123
  411.2 9.9 copy-start.126
  447.3 16.4 %collective-permute-start.3 = (bf16[2,197,192]{2,1,0:T(8,128)(2,1)}, bf16[2,197,192]{2,1,0:T(8,128)(2,1)}, u32[]{:S(2)}, u32[]{:S(2)}) collective-permute-start(bf16[2,197,192]{2,1,0:T(8,128)(2,1)} %get-tuple-element.169), channel_id=1, source_target_pairs={{0,1},{1,2},{2,3},{3,0},{4,5},{5,6},{6,7},{7,4},{8,9},{9,10},{10,1... | collective-permute-start | bytes 453896 | tf_op jit(solution)/shard_map/ppermute | solution.py:18
  447.3 18.2 %collective-permute-start.4 = (bf16[2,197,192]{2,1,0:T(8,128)(2,1)}, bf16[2,197,192]{2,1,0:T(8,128)(2,1)}, u32[]{:S(2)}, u32[]{:S(2)}) collective-permute-start(bf16[2,197,192]{2,1,0:T(8,128)(2,1)} %get-tuple-element.169), channel_id=1, source_target_pairs={{0,3},{1,0},{2,1},{3,2},{4,7},{5,4},{6,5},{7,6},{8,11},{9,8},{10,9... | collective-permute-start | bytes 453896 | tf_op jit(solution)/shard_map/ppermute | solution.py:21
  453.3 35.8 %collective-permute-start.9 = (bf16[1,512,192]{2,1,0:T(8,128)(2,1)}, bf16[1,512,192]{2,1,0:T(8,128)(2,1)}, u32[]{:S(2)}, u32[]{:S(2)}) collective-permute-start(bf16[1,512,192]{2,1,0:T(8,128)(2,1)} %get-tuple-element.171), channel_id=1, source_target_pairs={{0,1},{1,2},{2,3},{3,0},{4,5},{5,6},{6,7},{7,4},{8,9},{9,10},{10,1... | collective-permute-start | bytes 589832 | tf_op jit(solution)/shard_map/ppermute | solution.py:18
  453.8 38.5 %collective-permute-start.10 = (bf16[1,512,192]{2,1,0:T(8,128)(2,1)}, bf16[1,512,192]{2,1,0:T(8,128)(2,1)}, u32[]{:S(2)}, u32[]{:S(2)}) collective-permute-start(bf16[1,512,192]{2,1,0:T(8,128)(2,1)} %get-tuple-element.171), channel_id=1, source_target_pairs={{0,3},{1,0},{2,1},{3,2},{4,7},{5,4},{6,5},{7,6},{8,11},{9,8},{10,9... | collective-permute-start | bytes 589832 | tf_op jit(solution)/shard_map/ppermute | solution.py:21
  463.7 33.4 %collective-permute-start.15 = (bf16[1,711,192]{2,1,0:T(8,128)(2,1)}, bf16[1,711,192]{2,1,0:T(8,128)(2,1)}, u32[]{:S(2)}, u32[]{:S(2)}) collective-permute-start(bf16[1,711,192]{2,1,0:T(8,128)(2,1)} %get-tuple-element.174), channel_id=1, source_target_pairs={{0,1},{1,2},{2,3},{3,0},{4,5},{5,6},{6,7},{7,4},{8,9},{9,10},{10,1... | collective-permute-start | bytes 819080 | tf_op jit(solution)/shard_map/ppermute | solution.py:18
  463.8 37.9 %collective-permute-start.16 = (bf16[1,711,192]{2,1,0:T(8,128)(2,1)}, bf16[1,711,192]{2,1,0:T(8,128)(2,1)}, u32[]{:S(2)}, u32[]{:S(2)}) collective-permute-start(bf16[1,711,192]{2,1,0:T(8,128)(2,1)} %get-tuple-element.174), channel_id=1, source_target_pairs={{0,3},{1,0},{2,1},{3,2},{4,7},{5,4},{6,5},{7,6},{8,11},{9,8},{10,9... | collective-permute-start | bytes 819080 | tf_op jit(solution)/shard_map/ppermute | solution.py:21
  465.5 41.3 %collective-permute-start.5 = (bf16[2,197,192]{2,1,0:T(8,128)(2,1)}, bf16[2,197,192]{2,1,0:T(8,128)(2,1)}, u32[]{:S(2)}, u32[]{:S(2)}) collective-permute-start(bf16[2,197,192]{2,1,0:T(8,128)(2,1)} %collective-permute-done.3), channel_id=1, source_target_pairs={{0,1},{1,2},{2,3},{3,0},{4,5},{5,6},{6,7},{7,4},{8,9},{9,10},{10,1... | collective-permute-start | bytes 453896 | tf_op jit(solution)/shard_map/ppermute | solution.py:18
  496.2 14.2 %copy-start.83 = (f32[2,3,197]{2,1,0:T(4,128)S(1)}, f32[2,3,197]{2,1,0:T(4,128)}, u32[]{:S(2)}) copy-start(f32[2,3,197]{2,1,0:T(4,128)} %copy-done.82) | copy-start | bytes 14188
  496.2 24.6 %collective-permute-start.11 = (bf16[1,512,192]{2,1,0:T(8,128)(2,1)}, bf16[1,512,192]{2,1,0:T(8,128)(2,1)}, u32[]{:S(2)}, u32[]{:S(2)}) collective-permute-start(bf16[1,512,192]{2,1,0:T(8,128)(2,1)} %collective-permute-done.9), channel_id=1, source_target_pairs={{0,1},{1,2},{2,3},{3,0},{4,5},{5,6},{6,7},{7,4},{8,9},{9,10},{10,1... | collective-permute-start | bytes 589832 | tf_op jit(solution)/shard_map/ppermute | solution.py:18
  506.8 30.6 %collective-permute-start.17 = (bf16[1,711,192]{2,1,0:T(8,128)(2,1)}, bf16[1,711,192]{2,1,0:T(8,128)(2,1)}, u32[]{:S(2)}, u32[]{:S(2)}) collective-permute-start(bf16[1,711,192]{2,1,0:T(8,128)(2,1)} %collective-permute-done.15), channel_id=1, source_target_pairs={{0,1},{1,2},{2,3},{3,0},{4,5},{5,6},{6,7},{7,4},{8,9},{9,10},{10,1... | collective-permute-start | bytes 819080 | tf_op jit(solution)/shard_map/ppermute | solution.py:18
  520.6 133.6 %reduce-scatter.37.cloned.1.call-start = ((), (), s32[]{:S(2)}) async-start(), calls=%async_computation.16 | async-start | bytes 983040
  537.4 119.0 %reduce-scatter.41.cloned.1.call-start = ((), (), s32[]{:S(2)}) async-start(), calls=%async_computation.18 | async-start | bytes 1474560
  548.1 10.0 copy-start.53
  569.3 152.2 %reduce-scatter.45.cloned.1.call-start = ((), (), s32[]{:S(2)}) async-start(), calls=%async_computation.20 | async-start | bytes 2211840
  580.0 220.1 %reduce-scatter.43.cloned.1.call-start = ((), (), s32[]{:S(2)}) async-start(), calls=%async_computation.19 | async-start | bytes 6193152
  609.7 322.6 %reduce-scatter.47.cloned.1.call-start = ((), (), s32[]{:S(2)}) async-start(), calls=%async_computation.21 | async-start | bytes 7962624
  638.1 426.6 %reduce-scatter.29.cloned.1.call-start = ((), (), s32[]{:S(2)}) async-start(), calls=%async_computation.12 | async-start | bytes 7962624 | tf_op jit(solution)/shard_map/reduce_scatter | solution.py:340
  655.8 17.2 %copy-start.33 = (bf16[2,197,192]{2,1,0:T(8,128)(2,1)S(1)}, bf16[2,197,192]{2,1,0:T(8,128)(2,1)}, u32[]{:S(2)}) copy-start(bf16[2,197,192]{2,1,0:T(8,128)(2,1)} %copy-done.32) | copy-start | bytes 453892
  655.8 17.2 %copy-start.34 = (bf16[2,197,192]{2,1,0:T(8,128)(2,1)S(1)}, bf16[2,197,192]{2,1,0:T(8,128)(2,1)}, u32[]{:S(2)}) copy-start(bf16[2,197,192]{2,1,0:T(8,128)(2,1)} %copy.206) | copy-start | bytes 453892
  655.8 17.2 %copy-start.117 = (f32[2,197]{1,0:T(2,128)S(1)}, f32[2,197]{1,0:T(2,128)}, u32[]{:S(2)}) copy-start(f32[2,197]{1,0:T(2,128)} %copy-done.116) | copy-start | bytes 4732
  655.8 17.2 %copy-start.135 = (f32[192]{0:T(256)S(1)}, f32[192]{0:T(256)}, u32[]{:S(2)}) copy-start(f32[192]{0:T(256)} %copy-done.134) | copy-start | bytes 2308
  655.8 17.2 %copy-start.157 = (f32[2,197]{1,0:T(2,128)S(1)}, f32[2,197]{1,0:T(2,128)}, u32[]{:S(2)}) copy-start(f32[2,197]{1,0:T(2,128)} %get-tuple-element.154) | copy-start | bytes 4732
  655.8 17.2 %copy-start.196 = (f32[1,192]{1,0:T(1,128)S(1)}, f32[1,192]{1,0:T(1,128)}, u32[]{:S(2)}) copy-start(f32[1,192]{1,0:T(1,128)} %get-tuple-element.216) | copy-start | bytes 2308
  658.5 19.7 %copy-start.43 = (f32[1,512,192]{2,1,0:T(8,128)S(1)}, f32[1,512,192]{2,1,0:T(8,128)}, u32[]{:S(2)}) copy-start(f32[1,512,192]{2,1,0:T(8,128)} %get-tuple-element.172) | copy-start | bytes 1179652
  (190 other events, 542.5 us)
Sparse Core Ops, SparseCore 0:
  51.2 37.0 all-reduce.14
  89.9 18.1 all-gather.10
  207.5 65.1 all-reduce.18
  296.5 23.2 reduce-scatter.34
  342.8 24.2 reduce-scatter.30
  369.6 26.0 reduce-scatter.38
  403.3 26.6 reduce-scatter.32
  520.7 44.5 all-reduce.16
  567.8 23.2 reduce-scatter.36
  593.5 25.6 reduce-scatter.40
  622.7 67.8 reduce-scatter.44
  694.0 105.9 reduce-scatter.42
  803.7 128.5 reduce-scatter.46
  936.4 128.2 reduce-scatter.28
